TPU v7x, 256 devices: a whole 4x4x8 slice. The times are simulated.
256 devices in a mesh: leaf: 64 (over z, y, core), hand: 4 (over x).
Axes of the slice: x: 4, y: 4, z: 8, core: 2. Of those that a mesh axis runs over, the one named last changes fastest.
Arguments:
- opp_range: float32 [1024], P('hand'), may hold values from 0.1 to 1
- br_range: float32 [1024], P('hand'), may hold values from 0.001 to 1
- up_weight: bfloat16 [4, 2048, 1024], P(None, 'leaf', 'hand'), may hold values from 0.29882812 to 1
- up_parent: int32 [3, 2048], replicated, may hold values from 0 to 2047
- board_cards: int32 [6144, 5], P('leaf'), may hold values from 0 to 51, as said below
- hand_rank: int32 [6144, 1024], P('leaf'), may hold values from 0 to 7461
- root_parent: int32 [6144], P('leaf'), may hold values from 0 to 2047
- br_actions: int32 [6144], P('leaf'), may hold values from 1 to 8
- opp_actions: int32 [6144, 8], P('leaf'), may hold values from 1 to 8
- leaf_kind: int32 [6144, 8, 8], P('leaf'), may hold values from 0 to 1
- leaf_stake: int32 [6144, 8, 8], P('leaf'), may hold values from 1 to 400
- opp_weight: bfloat16 [6144, 8, 8, 1024], P('leaf', None, None, 'hand'), may hold values from 0.049804688 to 1
Outputs:
- level_values: float32 [4, 2048, 1024], P(None, 'leaf', 'hand')
- root_value: float32 [1024], P('hand')
- best_value: float32 [], replicated
Inputs may be any that keep to these rules, and one draw needn't show every extreme that they name: `board_cards`: five different cards for each subtree.
All inputs are finite; a program needn't handle non-finite values.
Results may differ from a plain program's by a relative error of at most 0.0003.
Values may be sent and summed in bfloat16 or wider, within the bound.
A program may use at most 128 MiB of HBM per device.

v0:
```python
import jax
import jax.numpy as jnp
import numpy as np
from jax import lax
from jax.sharding import Mesh
from jax.sharding import PartitionSpec as P

LEAF = ("leaf_0", "leaf_1", "leaf_2")
PAYOFF_UNIT = 1.0 / 4096.0


def laid_out(parts, dim):
    parts = jnp.moveaxis(parts, 0, dim)
    lengths = parts.shape
    return parts.reshape(*lengths[:dim], lengths[dim] * lengths[dim + 1], *lengths[dim + 2 :])


def all_blocks(x, axes, turns):
    parts = x[None]
    for k in turns:
        parts = lax.all_gather(parts, axes[k], axis=0, tiled=True)
    carried = [lax.axis_size(axes[k]) for k in reversed(turns)]
    parts = parts.reshape(*carried, *x.shape)
    turned = sorted(range(len(turns)), key=lambda place: turns[len(turns) - 1 - place])
    return parts.transpose(*turned, *range(len(turns), parts.ndim)).reshape(-1, *x.shape)


def whole_of(x, axes, turns, dim):
    return laid_out(all_blocks(x, axes, turns), dim)


def split_up(x, dim, devices):
    before, after = (x.shape[:dim], x.shape[dim + 1 :])
    return jnp.moveaxis(x.reshape(*before, devices, -1, *after), dim, 0)


def summed_on_arrival(x, axis, dim):
    parts = split_up(x, dim, lax.axis_size(axis))
    arrived = lax.all_to_all(parts, axis, split_axis=0, concat_axis=0, tiled=True)
    return arrived.sum(axis=0)


def copy_for_each(x, axis):
    devices = lax.axis_size(axis)
    return lax.all_to_all(jnp.broadcast_to(x[None], (devices, *x.shape)), axis, 0, 0, tiled=True)


def gather_directly(x, axis, dim):
    return laid_out(copy_for_each(x, axis), dim)


def of_everyone(x, axis):
    everything = copy_for_each(x, axis)
    return jnp.sum(everything, axis=0)


def hand_cards(number):
    low_list = []
    high_list = []
    for low_card in range(52):
        for high_card in range(low_card + 1, 52):
            low_list.append(low_card)
            high_list.append(high_card)
    chosen = np.arange(number) * 1326 // number
    return (np.array(low_list, np.int32)[chosen], np.array(high_list, np.int32)[chosen])


def no_shared(low_rows, high_rows, low_cols, high_cols):
    apart_mask = (low_rows[:, None] != low_cols[None, :]) & (
        low_rows[:, None] != high_cols[None, :]
    )
    apart_mask = (
        apart_mask
        & (high_rows[:, None] != low_cols[None, :])
        & (high_rows[:, None] != high_cols[None, :])
    )
    return apart_mask.astype(jnp.float32)


def board_compat(board_cards, low_cols, high_cols):
    hits = (board_cards[:, :, None] == low_cols[None, None, :]) | (
        board_cards[:, :, None] == high_cols[None, None, :]
    )
    return 1.0 - jnp.any(hits, axis=1).astype(jnp.float32)


def local(
    opp_range,
    br_range,
    up_weight,
    up_parent,
    board_cards,
    hand_rank,
    root_parent,
    br_actions,
    opp_actions,
    leaf_kind,
    leaf_stake,
    opp_weight,
):
    levels_count = up_weight.shape[0]
    nodes_dev = up_weight.shape[1]
    hands_dev = opp_range.shape[0]
    boards_dev = board_cards.shape[0]
    actions_max = opp_actions.shape[1]
    hands_all = hand_rank.shape[1]
    node_total = nodes_dev * lax.axis_size(LEAF)
    node_start = lax.axis_index(LEAF) * nodes_dev
    hand_start = lax.axis_index("hand") * hands_dev
    low_np, high_np = hand_cards(hands_all)
    low_all = jnp.asarray(low_np)
    high_all = jnp.asarray(high_np)
    low_mine = lax.dynamic_slice_in_dim(low_all, hand_start, hands_dev)
    high_mine = lax.dynamic_slice_in_dim(high_all, hand_start, hands_dev)
    compat = board_compat(board_cards, low_mine, high_mine)
    weights = whole_of(up_weight, LEAF, (1, 0, 2), 1)
    gathered = opp_range[None, :] * weights[0].astype(jnp.float32)
    for level_id in range(1, levels_count):
        gathered = jnp.take(gathered, up_parent[level_id - 1], axis=0) * weights[level_id].astype(
            jnp.float32
        )
    root_reach = jnp.take(gathered, root_parent, axis=0) * compat
    legal_mask = (jnp.arange(actions_max)[None, None, :] < opp_actions[:, :, None]).astype(
        jnp.float32
    )
    weighted = opp_weight.astype(jnp.float32) * legal_mask[..., None]
    probability = weighted / jnp.sum(weighted, axis=2, keepdims=True)
    leaf_reach = (root_reach[:, None, None, :] * probability).astype(jnp.bfloat16)
    leaf_reach = leaf_reach.reshape(boards_dev, actions_max * actions_max, hands_dev)
    kind_flat = leaf_kind.reshape(boards_dev, -1)
    stake_flat = leaf_stake.reshape(boards_dev, -1).astype(jnp.float32) * PAYOFF_UNIT
    rank_mine = lax.dynamic_slice_in_dim(hand_rank, hand_start, hands_dev, 1)
    zero_block = jnp.zeros(leaf_reach.shape, jnp.float32)
    block_rows = lax.all_gather(leaf_reach, "hand", axis=2, tiled=True)
    count_rows = block_rows.shape[2]
    low_rows = lax.slice_in_dim(low_all, 0, count_rows, axis=0)
    high_rows = lax.slice_in_dim(high_all, 0, count_rows, axis=0)
    apart_mask = no_shared(low_rows, high_rows, low_mine, high_mine).astype(jnp.bfloat16)
    order_sign = (
        jnp.sign(rank_mine[:, None, :] - hand_rank[:, :, None]).astype(jnp.bfloat16)
        * apart_mask[None]
    )
    showdown = zero_block + jnp.einsum(
        "blo,boh->blh", block_rows, order_sign, preferred_element_type=jnp.float32
    )
    folded = zero_block + jnp.einsum(
        "blo,oh->blh", block_rows, apart_mask, preferred_element_type=jnp.float32
    )
    showdown, folded = (showdown, folded)
    payoff = (
        jnp.where(kind_flat[:, :, None] == 1, showdown, folded)
        * stake_flat[:, :, None]
        * compat[:, None, :]
    )
    per_node = jnp.sum(payoff.reshape(boards_dev, actions_max, actions_max, hands_dev), axis=2)
    allowed = jnp.arange(actions_max)[None, :, None] < br_actions[:, None, None]
    sub_value = jnp.max(jnp.where(allowed, per_node, -1e30), axis=1)
    contrib = jax.ops.segment_sum(sub_value, root_parent, num_segments=node_total)
    last_mine = summed_on_arrival(contrib, LEAF, 0)
    whole_level = gather_directly(last_mine, LEAF, 0)
    level_list = [last_mine]
    for level_id in range(levels_count - 1, 0, -1):
        whole_level = jax.ops.segment_sum(
            whole_level, up_parent[level_id - 1], num_segments=node_total
        )
        level_list.insert(0, lax.dynamic_slice_in_dim(whole_level, node_start, nodes_dev))
    level_values = jnp.stack(level_list)
    local_total = jnp.sum(level_values[0], axis=0)
    root_value = of_everyone(local_total, LEAF) / node_total
    weighted_sum, range_total = lax.psum(
        (jnp.sum(br_range * root_value), jnp.sum(br_range)), "hand"
    )
    best_value = weighted_sum / range_total
    return (level_values, root_value, best_value)


def solution(mesh):
    split = Mesh(
        mesh.devices.reshape(8, 4, 2, mesh.shape["hand"]), ("leaf_0", "leaf_1", "leaf_2", "hand")
    )
    in_specs = (
        P("hand"),
        P("hand"),
        P(None, LEAF, "hand"),
        P(),
        P(LEAF, None),
        P(LEAF, None),
        P(LEAF),
        P(LEAF),
        P(LEAF, None),
        P(LEAF, None, None),
        P(LEAF, None, None),
        P(LEAF, None, None, "hand"),
    )
    out_specs = (P(None, LEAF, "hand"), P("hand"), P())
    return jax.shard_map(local, mesh=split, in_specs=in_specs, out_specs=out_specs, check_vma=False)
```

profile of v0, /device:TPU:1, one launch (start us, length us, event | category | flops | bytes accessed | tf_op | source)
XLA Modules:
  0.0 494.6 jit_solution(5926093371873539124)
XLA Ops:
  7.3 12.7 %all-gather = bf16[16,32,256]{2,1,0:T(8,128)(2,1)} all-gather(bf16[4,32,256]{2,1,0:T(8,128)(2,1)} %param.18), channel_id=2, replica_groups=mesh['leaf_0'=8,'leaf_1'=4,'leaf_2'=2,'hand'=4] {'leaf_1'}, dimensions={0}, use_global_device_ids=true | all-gather | bytes 327680 | tf_op jit(solution)/shard_map/all_gather | solution.py:21
  20.0 40.9 %all-gather.5.cloned.1.call-done = bf16[32,4,32,256]{3,2,1,0:T(8,128)(2,1)} async-done(((bf16[4,4,32,256]{3,2,1,0:T(8,128)(2,1)}), bf16[32,4,32,256]{3,2,1,0:T(8,128)(2,1)}) %all-gather.5.cloned.1.call-update) | async-done | bytes 2097168 | tf_op jit(solution)/shard_map/all_gather | solution.py:21
  63.2 0.8 or_reduce_fusion
  68.3 16.9 %all-gather.7.cloned.1.call-done = bf16[64,4,32,256]{3,2,1,0:T(8,128)(2,1)} async-done(((bf16[32,4,32,256]{3,2,1,0:T(8,128)(2,1)}), bf16[64,4,32,256]{3,2,1,0:T(8,128)(2,1)}) %all-gather.7.cloned.1.call-update) | async-done | bytes 4194320 | tf_op jit(solution)/shard_map/all_gather | solution.py:21
  85.2 2.6 copy.32
  87.9 1.7 fusion.27
  89.8 9.3 %gather_fusion.1 = f32[2048,256]{1,0:T(8,128)} fusion(f32[2048,256]{1,0:T(8,128)S(1)} %convert_multiply_fusion.5, s32[2048]{0:T(1024)} %fusion.23), kind=kCustom, calls=%fused_computation.clone | custom fusion | bytes 4202496 | tf_op jit(solution)/shard_map/jit(_take)/gather | solution.py:119
  99.1 2.1 convert_multiply_fusion.4
  101.3 9.3 %gather_fusion.2 = f32[2048,256]{1,0:T(8,128)} fusion(f32[2048,256]{1,0:T(8,128)S(1)} %convert_multiply_fusion.4, s32[2048]{0:T(1024)} %fusion.24), kind=kCustom, calls=%fused_computation.1.clone | custom fusion | bytes 4202496 | tf_op jit(solution)/shard_map/jit(_take)/gather | solution.py:119
  110.5 2.1 convert_multiply_fusion.3
  112.7 9.3 %gather_fusion.3 = f32[2048,256]{1,0:T(8,128)} fusion(f32[2048,256]{1,0:T(8,128)S(1)} %convert_multiply_fusion.3, s32[2048]{0:T(1024)} %fusion.25), kind=kCustom, calls=%fused_computation.2.clone | custom fusion | bytes 4202496 | tf_op jit(solution)/shard_map/jit(_take)/gather | solution.py:119
  122.0 1.8 convert_multiply_fusion.2
  123.8 0.8 gather_fusion
  124.6 0.8 convert_subtract_fusion
  125.4 6.9 %fusion.9 = bf16[96,64,256]{2,1,0:T(8,128)(2,1)} fusion(f32[96,8,8]{2,1,0:T(8,128)S(1)} %fusion.22, bf16[96,8,8,256]{3,2,1,0:T(8,128)(2,1)} %param.27, f32[96,256]{1,0:T(8,128)S(1)} %get-tuple-element.19), kind=kOutput, calls=%fused_computation.20 | output fusion | flops 11206663 | bytes 6414336 | tf_op jit(solution)/shard_map/div | solution.py:127
  134.2 122.0 %all-gather.9.cloned.1.call-done = bf16[96,64,1024]{2,1,0:T(8,128)(2,1)} async-done(((bf16[96,64,256]{2,1,0:T(8,128)(2,1)}), bf16[96,64,1024]{2,1,0:T(8,128)(2,1)}) %all-gather.9.cloned.1.call-update) | async-done | bytes 12582928 | tf_op jit(solution)/shard_map/all_gather | solution.py:134
  256.3 8.5 %fusion.20 = f32[96,64,256]{2,1,0:T(8,128)S(1)} fusion(bf16[96,64,1024]{2,1,0:T(8,128)(2,1)} %all-gather.9.cloned.1.call-done, s32[256]{0:T(256)S(1)} %copy-done.9, s32[256]{0:T(256)S(1)} %copy-done.7, s32[1024]{0:T(1024)S(1)} %copy-done.11, s32[1024]{0:T(1024)S(1)} %copy-done.10), kind=kOutput, calls=%fused_computation.35 | convolution fusion | flops 3223584768 | bytes 18884608 | tf_op jit(solution)/shard_map/blo,oh->blh/dot_general | solution.py:146
  264.8 28.5 %bitcast_reduce_fusion = f32[96,8,256]{2,1,0:T(8,128)S(1)} fusion(f32[96,64,256]{2,1,0:T(8,128)S(1)} %fusion.20, f32[96,256]{1,0:T(8,128)S(1)} %get-tuple-element.18, f32[96,64]{1,0:T(8,128)S(1)} %copy.34, pred[96,64]{1,0:T(8,128)(4,1)S(1)} %copy.31, bf16[96,64,1024]{2,1,0:T(8,128)(2,1)S(1)} %copy-done.17, s32[96,1024]{1,0:T(8,128)S(1)} %copy-done.4, ...), kind=kOutput, calls=%fused_computation.15 | convolution fusion | flops 3327983616 | bytes 20805632 | tf_op jit(solution)/shard_map/blo,boh->blh/dot_general | solution.py:143
  293.6 1.7 scatter_custom_fusion
  295.3 62.1 %all_to_all.16 = f32[64,32,256]{2,1,0:T(8,128)} all-to-all(f32[64,32,256]{2,1,0:T(8,128)S(1)} %bitcast.47), channel_id=1, replica_groups=mesh['leaf_0'=8,'leaf_1'=4,'leaf_2'=2,'hand'=4] {'leaf_0','leaf_1','leaf..., dimensions={0} | all-to-all | bytes 4194304 | tf_op jit(solution)/shard_map/all_to_all | solution.py:39
  357.4 1.7 reduce_sum.65
  359.1 1.6 broadcast_in_dim.59
  360.7 7.0 %all-to-all-start.1 = ((f32[64,32,256]{2,1,0:T(8,128)}), f32[64,32,256]{2,1,0:T(8,128)S(1)}, u32[]{:S(2)}, u32[]{:S(2)}) async-start(f32[64,32,256]{2,1,0:T(8,128)} %broadcast_in_dim.59), calls=%async_computation.1 | async-start | bytes 4194304 | tf_op jit(solution)/shard_map/all_to_all | solution.py:45
  367.7 49.7 %all-to-all-done.1 = f32[64,32,256]{2,1,0:T(8,128)S(1)} async-done(((f32[64,32,256]{2,1,0:T(8,128)}), f32[64,32,256]{2,1,0:T(8,128)S(1)}, u32[]{:S(2)}, u32[]{:S(2)}) %all-to-all-start.1) | async-done | bytes 2097184 | tf_op jit(solution)/shard_map/all_to_all | solution.py:45
  417.4 1.3 copy-done
  418.7 12.5 %scatter_custom_fusion.1 = f32[2048,256]{1,0:T(8,128)S(1)} fusion(s32[2048]{0:T(1024)} %bitcast.60, f32[2048,256]{1,0:T(8,128)} %bitcast.49, f32[]{:T(128)} %constant.20.clone.1), kind=kCustom, calls=%fused_computation.30 | custom fusion | flops 524288 | bytes 2097664 | tf_op jit(solution)/shard_map/scatter-add | solution.py:163
  431.2 13.0 %scatter_custom_fusion.2 = f32[2048,256]{1,0:T(8,128)} fusion(s32[2048]{0:T(1024)S(1)} %bitcast.57, f32[2048,256]{1,0:T(8,128)S(1)} %scatter_custom_fusion.1, f32[]{:T(128)} %constant.20.clone.1), kind=kCustom, calls=%fused_computation.28 | custom fusion | flops 524288 | bytes 2097156 | tf_op jit(solution)/shard_map/scatter-add | solution.py:163
  444.2 13.3 %scatter_custom_fusion.3 = f32[2048,256]{1,0:T(8,128)} fusion(s32[2048]{0:T(1024)S(1)} %bitcast.54, f32[2048,256]{1,0:T(8,128)} %scatter_custom_fusion.2, f32[]{:T(128)} %constant.20.clone.1), kind=kCustom, calls=%fused_computation.26 | custom fusion | flops 524288 | bytes 2097664 | tf_op jit(solution)/shard_map/scatter-add | solution.py:163
  459.0 7.0 %all-to-all-start.2 = ((f32[64,1,256]{2,1,0:T(1,128)}), f32[64,1,256]{2,1,0:T(1,128)S(1)}, u32[]{:S(2)}, u32[]{:S(2)}) async-start(f32[64,1,256]{2,1,0:T(1,128)} %broadcast_in_dim.96), calls=%async_computation.2 | async-start | bytes 131072 | tf_op jit(solution)/shard_map/all_to_all | solution.py:45
  467.4 8.6 %all-to-all-done.2 = f32[64,1,256]{2,1,0:T(1,128)S(1)} async-done(((f32[64,1,256]{2,1,0:T(1,128)}), f32[64,1,256]{2,1,0:T(1,128)S(1)}, u32[]{:S(2)}, u32[]{:S(2)}) %all-to-all-start.2) | async-done | bytes 65568 | tf_op jit(solution)/shard_map/all_to_all | solution.py:45
  476.1 1.2 fusion.26
  477.3 8.4 %all-reduce = (f32[]{:T(128)}, f32[]{:T(128)}) all-reduce(f32[]{:T(128)} %get-tuple-element.5, f32[]{:T(128)} %get-tuple-element.4), channel_id=1, replica_groups=mesh['leaf_0'=8,'leaf_1'=4,'leaf_2'=2,'hand'=4] {'hand'}, use_global_device_ids=true, to_apply=%region_12.14 | all-reduce | flops 2 | bytes 16 | tf_op jit(solution)/shard_map/psum | solution.py:170
  (71 shorter events, 12.0 us)
Async XLA Ops:
  7.2 55.4 %copy-start.13 = (s32[96,8]{0,1:T(8,128)S(1)}, s32[96,8]{0,1:T(8,128)}, u32[]{:S(2)}) copy-start(s32[96,8]{0,1:T(8,128)} %param.24) | copy-start | bytes 9220
  7.2 55.4 %copy-start.18 = (s32[96]{0:T(128)S(1)}, s32[96]{0:T(128)}, u32[]{:S(2)}) copy-start(s32[96]{0:T(128)} %param.22) | copy-start | bytes 1156
  7.2 56.0 %copy-start.12 = (s32[96,5]{0,1:T(8,128)S(1)}, s32[96,5]{0,1:T(8,128)}, u32[]{:S(2)}) copy-start(s32[96,5]{0,1:T(8,128)} %param.20) | copy-start | bytes 5764
  7.2 57.4 %copy-start.5 = (s32[3,2048]{1,0:T(4,128)S(1)}, s32[3,2048]{1,0:T(4,128)}, u32[]{:S(2)}) copy-start(s32[3,2048]{1,0:T(4,128)} %param.19) | copy-start | bytes 73732
  7.2 53.7 %all-gather.5.cloned.1.call-start = ((), (), s32[]{:S(2)}) async-start(), calls=%async_computation.3 | async-start | bytes 2359296 | tf_op jit(solution)/shard_map/all_gather | solution.py:21
  19.9 65.3 %all-gather.7.cloned.1.call-start = ((), (), s32[]{:S(2)}) async-start(), calls=%async_computation.4 | async-start | bytes 6291456 | tf_op jit(solution)/shard_map/all_gather | solution.py:21
  60.9 195.3 %all-gather.9.cloned.1.call-start = ((), (), s32[]{:S(2)}) async-start(), calls=%async_computation.5 | async-start | bytes 15728640 | tf_op jit(solution)/shard_map/all_gather | solution.py:134
  61.8 2.3 copy-start.6
  62.5 1.5 copy-start.8
  64.6 23.3 %copy-start.1 = (s32[1,2048]{1,0:T(1,128)}, s32[1,2048]{1,0:T(1,128)S(1)}, u32[]{:S(2)}) copy-start(s32[1,2048]{1,0:T(1,128)S(1)} %get-tuple-element.15) | copy-start | bytes 24580
  87.9 1.8 copy-start.14
  132.3 0.8 copy-start.3
  132.3 0.9 copy-start.2
  132.3 1.0 copy-start.4
  132.3 1.0 copy-start.16
  132.3 1.1 copy-start.7
  132.4 1.1 copy-start.9
  132.4 1.1 copy-start.10
  132.4 1.1 copy-start.11
  256.3 8.5 %copy-start.17 = (bf16[96,64,1024]{2,1,0:T(8,128)(2,1)S(1)}, bf16[96,64,1024]{2,1,0:T(8,128)(2,1)}, u32[]{:S(2)}) copy-start(bf16[96,64,1024]{2,1,0:T(8,128)(2,1)} %all-gather.9.cloned.1.call-done) | copy-start | bytes 37748740
  360.7 56.7 %all-to-all-start.1 = ((f32[64,32,256]{2,1,0:T(8,128)}), f32[64,32,256]{2,1,0:T(8,128)S(1)}, u32[]{:S(2)}, u32[]{:S(2)}) async-start(f32[64,32,256]{2,1,0:T(8,128)} %broadcast_in_dim.59), calls=%async_computation.1 | async-start | bytes 4194304 | tf_op jit(solution)/shard_map/all_to_all | solution.py:45
  417.4 1.4 copy-start
  431.2 44.9 %copy-start.15 = (f32[256]{0:T(256)S(1)}, f32[256]{0:T(256)}, u32[]{:S(2)}) copy-start(f32[256]{0:T(256)} %param.17) | copy-start | bytes 3076
  459.0 17.0 %all-to-all-start.2 = ((f32[64,1,256]{2,1,0:T(1,128)}), f32[64,1,256]{2,1,0:T(1,128)S(1)}, u32[]{:S(2)}, u32[]{:S(2)}) async-start(f32[64,1,256]{2,1,0:T(1,128)} %broadcast_in_dim.96), calls=%async_computation.2 | async-start | bytes 131072 | tf_op jit(solution)/shard_map/all_to_all | solution.py:45
Sparse Core Ops, SparseCore 0:
  20.1 40.8 all-gather.4
  62.7 22.4 all-gather.6
  132.5 123.6 all-gather.8
where the time goes:
time: 496 us; the launch traced here: 495 us
  waiting for transfers between devices  238 us (48%)
  blocking collectives  83.1 us (17%)
  other arithmetic  65.8 us (13%)
  local copies, waits for them, and re-layouts  40.1 us (8%)
  matrix products  37 us (7%)
  between operations  16.5 us (3%)
  starting transfers between devices  14 us (3%)
    all_gather x1, waiting for transfers between devices, local(): block_rows = lax.all_gather(leaf_reach, 'hand', axis=2, tiled=True)  122 us
    all_to_all x1, blocking collectives, summed_on_arrival(): lax.all_to_all(parts, axis, split_axis=0, concat_axis=0, tiled=True)  62.1 us
    all_to_all x2, waiting for transfers between devices, copy_for_each(): lax.all_to_all(jnp.broadcast_to(x[None], (devices, *x.shape)), axis, 0, 0...  58.3 us
    all_gather x2, waiting for transfers between devices, all_blocks(): parts = lax.all_gather(parts, axes[k], axis=0, tiled=True)  57.8 us
    scatter-add x3, other arithmetic, local(): jax.ops.segment_sum(whole_level, up_parent[level_id - 1], num_segments=no...  38.8 us
    dot_general x1, matrix products, local(): jnp.einsum('blo,boh->blh', block_rows, order_sign, preferred_element_type...  28.5 us
    gather x3, local copies, waits for them, and re-layouts, local(): jnp.take(gathered, up_parent[level_id - 1], axis=0)  27.9 us
    all_to_all x2, starting transfers between devices, copy_for_each(): lax.all_to_all(jnp.broadcast_to(x[None], (devices, *x.shape)), axis, 0, 0...  13.9 us
  transfers between devices with their start and end apart: 5, of which 5 were waited for; matrix products, arithmetic and copies ran while one was open for 2% of the time, Pallas kernels for 0%

commit v1 on v0

--- a/solution.py
+++ b/solution.py
@@ -98,6 +98,15 @@
     leaf_stake,
     opp_weight,
 ):
+
+    def tiles_choose(page):
+        grid = []
+        n_all = lax.axis_size("hand")
+        for c in [*range(page.ndim)]:
+            grid.append(n_all if c == 2 else 1)
+        current_value = jnp.tile(page, grid)
+        return lax.all_to_all(current_value, "hand", tiled=True, concat_axis=2, split_axis=2)
+
     levels_count = up_weight.shape[0]
     nodes_dev = up_weight.shape[1]
     hands_dev = opp_range.shape[0]
@@ -131,7 +140,7 @@
     stake_flat = leaf_stake.reshape(boards_dev, -1).astype(jnp.float32) * PAYOFF_UNIT
     rank_mine = lax.dynamic_slice_in_dim(hand_rank, hand_start, hands_dev, 1)
     zero_block = jnp.zeros(leaf_reach.shape, jnp.float32)
-    block_rows = lax.all_gather(leaf_reach, "hand", axis=2, tiled=True)
+    block_rows = tiles_choose(leaf_reach)
     count_rows = block_rows.shape[2]
     low_rows = lax.slice_in_dim(low_all, 0, count_rows, axis=0)
     high_rows = lax.slice_in_dim(high_all, 0, count_rows, axis=0)

time: 496 us -> 599 us (1.21)
  waiting for transfers between devices: 238 us -> 298 us
  local copies, waits for them, and re-layouts: 40.1 us -> 77.5 us
  starting transfers between devices: 14 us -> 21.3 us
    all_to_all x0 -> x1, waiting for transfers between devices: none -> 182 us  [tiles_choose(): lax.all_to_all(current_value, 'hand', tiled=True, concat_axis=2, split_ax...]
    all_gather x1 -> x0, waiting for transfers between devices: 122 us -> none  [local(): block_rows = lax.all_gather(leaf_reach, 'hand', axis=2, tiled=True)]
    all_to_all x0 -> x1, local copies, waits for them, and re-layouts: none -> 25 us  [tiles_choose(): lax.all_to_all(current_value, 'hand', tiled=True, concat_axis=2, split_ax...]
    another operation x0 -> x2, local copies, waits for them, and re-layouts: none -> 13.1 us  [tiles_choose(): current_value = jnp.tile(page, grid)]
    all_to_all x0 -> x1, starting transfers between devices: none -> 7.28 us  [tiles_choose(): lax.all_to_all(current_value, 'hand', tiled=True, concat_axis=2, split_ax...]
where the time goes in v1:
time: 599 us; the launch traced here: 597 us
  waiting for transfers between devices  298 us (50%)
  blocking collectives  80.6 us (13%)
  local copies, waits for them, and re-layouts  77.5 us (13%)
  other arithmetic  65.1 us (11%)
  matrix products  37 us (6%)
  starting transfers between devices  21.3 us (4%)
  between operations  16.8 us (3%)
    all_to_all x1, waiting for transfers between devices, tiles_choose(): lax.all_to_all(current_value, 'hand', tiled=True, concat_axis=2, split_ax...  182 us
    all_to_all x1, blocking collectives, summed_on_arrival(): lax.all_to_all(parts, axis, split_axis=0, concat_axis=0, tiled=True)  60.4 us
    all_to_all x2, waiting for transfers between devices, copy_for_each(): lax.all_to_all(jnp.broadcast_to(x[None], (devices, *x.shape)), axis, 0, 0...  58.3 us
    all_gather x2, waiting for transfers between devices, all_blocks(): parts = lax.all_gather(parts, axes[k], axis=0, tiled=True)  57.9 us
    scatter-add x3, other arithmetic, local(): jax.ops.segment_sum(whole_level, up_parent[level_id - 1], num_segments=no...  38.8 us
    dot_general x1, matrix products, local(): jnp.einsum('blo,boh->blh', block_rows, order_sign, preferred_element_type...  28.5 us
    gather x3, local copies, waits for them, and re-layouts, local(): jnp.take(gathered, up_parent[level_id - 1], axis=0)  27.9 us
    all_to_all x1, local copies, waits for them, and re-layouts, tiles_choose(): lax.all_to_all(current_value, 'hand', tiled=True, concat_axis=2, split_ax...  25 us
  transfers between devices with their start and end apart: 5, of which 5 were waited for; matrix products, arithmetic and copies ran while one was open for 2% of the time, Pallas kernels for 0%

profile of v1, /device:TPU:1, one launch (start us, length us, event | category | flops | bytes accessed | tf_op | source)
XLA Modules:
  0.0 596.8 jit_solution(458986123444705487)
XLA Ops:
  7.3 12.7 %all-gather = bf16[16,32,256]{2,1,0:T(8,128)(2,1)} all-gather(bf16[4,32,256]{2,1,0:T(8,128)(2,1)} %param.18), channel_id=2, replica_groups=mesh['leaf_0'=8,'leaf_1'=4,'leaf_2'=2,'hand'=4] {'leaf_1'}, dimensions={0}, use_global_device_ids=true | all-gather | bytes 327680 | tf_op jit(solution)/shard_map/all_gather | solution.py:21
  20.0 40.9 %all-gather.4.cloned.1.call-done = bf16[32,4,32,256]{3,2,1,0:T(8,128)(2,1)} async-done(((bf16[4,4,32,256]{3,2,1,0:T(8,128)(2,1)}), bf16[32,4,32,256]{3,2,1,0:T(8,128)(2,1)}) %all-gather.4.cloned.1.call-update) | async-done | bytes 2097168 | tf_op jit(solution)/shard_map/all_gather | solution.py:21
  68.2 17.0 %all-gather.6.cloned.1.call-done = bf16[64,4,32,256]{3,2,1,0:T(8,128)(2,1)} async-done(((bf16[32,4,32,256]{3,2,1,0:T(8,128)(2,1)}), bf16[64,4,32,256]{3,2,1,0:T(8,128)(2,1)}) %all-gather.6.cloned.1.call-update) | async-done | bytes 4194320 | tf_op jit(solution)/shard_map/all_gather | solution.py:21
  85.2 2.6 copy.46
  87.9 1.7 fusion.27
  89.8 9.3 %gather_fusion.1 = f32[2048,256]{1,0:T(8,128)} fusion(f32[2048,256]{1,0:T(8,128)S(1)} %convert_multiply_fusion.5, s32[2048]{0:T(1024)} %fusion.23), kind=kCustom, calls=%fused_computation.clone | custom fusion | bytes 4202496 | tf_op jit(solution)/shard_map/jit(_take)/gather | solution.py:128
  99.1 2.1 convert_multiply_fusion.4
  101.3 9.3 %gather_fusion.2 = f32[2048,256]{1,0:T(8,128)} fusion(f32[2048,256]{1,0:T(8,128)S(1)} %convert_multiply_fusion.4, s32[2048]{0:T(1024)} %fusion.24), kind=kCustom, calls=%fused_computation.1.clone | custom fusion | bytes 4202496 | tf_op jit(solution)/shard_map/jit(_take)/gather | solution.py:128
  110.5 2.1 convert_multiply_fusion.3
  112.7 9.3 %gather_fusion.3 = f32[2048,256]{1,0:T(8,128)} fusion(f32[2048,256]{1,0:T(8,128)S(1)} %convert_multiply_fusion.3, s32[2048]{0:T(1024)} %fusion.25), kind=kCustom, calls=%fused_computation.2.clone | custom fusion | bytes 4202496 | tf_op jit(solution)/shard_map/jit(_take)/gather | solution.py:128
  122.0 1.8 convert_multiply_fusion.2
  124.6 1.4 convert_subtract_fusion
  126.0 5.7 fusion.9
  131.7 5.4 copy.48
  137.1 7.7 %tile.11 = bf16[96,64,4,256]{0,1,3,2:T(8,128)(2,1)} broadcast(bf16[96,64,256]{0,1,2:T(8,128)(2,1)} %copy.48), dimensions={0,1,3} | broadcast | bytes 15728640 | tf_op jit(solution)/shard_map/tile | solution.py:107
  144.9 7.3 %all-to-all-start = ((bf16[96,64,1024]{0,1,2:T(8,128)(2,1)}), bf16[96,64,1024]{0,1,2:T(8,128)(2,1)}, u32[]{:S(2)}, u32[]{:S(2)}) async-start(bf16[96,64,1024]{0,1,2:T(8,128)(2,1)} %bitcast.47), calls=%async_computation | async-start | bytes 33554432 | tf_op jit(solution)/shard_map/all_to_all | solution.py:108
  153.4 182.2 %all-to-all-done = bf16[96,64,1024]{0,1,2:T(8,128)(2,1)} async-done(((bf16[96,64,1024]{0,1,2:T(8,128)(2,1)}), bf16[96,64,1024]{0,1,2:T(8,128)(2,1)}, u32[]{:S(2)}, u32[]{:S(2)}) %all-to-all-start) | async-done | bytes 12582944 | tf_op jit(solution)/shard_map/all_to_all | solution.py:108
  335.6 25.0 %copy.49 = bf16[96,64,1024]{2,1,0:T(8,128)(2,1)} copy(bf16[96,64,1024]{0,1,2:T(8,128)(2,1)} %all-to-all-done) | data formatting | bytes 25165824 | tf_op jit(solution)/shard_map/all_to_all | solution.py:108
  360.6 8.5 %fusion.20 = f32[96,64,256]{2,1,0:T(8,128)S(1)} fusion(bf16[96,64,1024]{2,1,0:T(8,128)(2,1)} %copy.49, s32[256]{0:T(256)S(1)} %copy-done.11, s32[256]{0:T(256)S(1)} %copy-done.9, s32[1024]{0:T(1024)S(1)} %copy-done.13, s32[1024]{0:T(1024)S(1)} %copy-done.12), kind=kOutput, calls=%fused_computation.35 | convolution fusion | flops 3223584768 | bytes 18884608 | tf_op jit(solution)/shard_map/blo,oh->blh/dot_general | solution.py:155
  369.1 28.5 %bitcast_reduce_fusion = f32[96,8,256]{2,1,0:T(8,128)S(1)} fusion(f32[96,64,256]{2,1,0:T(8,128)S(1)} %fusion.20, f32[96,256]{1,0:T(8,128)S(1)} %copy-done.2, f32[96,64]{1,0:T(8,128)S(1)} %copy.51, pred[96,64]{1,0:T(8,128)(4,1)S(1)} %copy.45, bf16[96,64,1024]{2,1,0:T(8,128)(2,1)S(1)} %copy-done, s32[96,1024]{1,0:T(8,128)S(1)} %copy-done.6, ...), kind=kOutput, calls=%fused_computation.15 | convolution fusion | flops 3327983616 | bytes 20805632 | tf_op jit(solution)/shard_map/blo,boh->blh/dot_general | solution.py:152
  397.9 1.7 scatter_custom_fusion
  399.7 60.4 %all_to_all.21 = f32[64,32,256]{2,1,0:T(8,128)} all-to-all(f32[64,32,256]{2,1,0:T(8,128)S(1)} %bitcast.49), channel_id=1, replica_groups=mesh['leaf_0'=8,'leaf_1'=4,'leaf_2'=2,'hand'=4] {'leaf_0','leaf_1','leaf..., dimensions={0} | all-to-all | bytes 4194304 | tf_op jit(solution)/shard_map/all_to_all | solution.py:39
  460.1 1.7 reduce_sum.65
  461.8 1.6 broadcast_in_dim.59
  463.4 7.0 %all-to-all-start.2 = ((f32[64,32,256]{2,1,0:T(8,128)}), f32[64,32,256]{2,1,0:T(8,128)S(1)}, u32[]{:S(2)}, u32[]{:S(2)}) async-start(f32[64,32,256]{2,1,0:T(8,128)} %broadcast_in_dim.59), calls=%async_computation.2 | async-start | bytes 4194304 | tf_op jit(solution)/shard_map/all_to_all | solution.py:45
  470.4 49.7 %all-to-all-done.2 = f32[64,32,256]{2,1,0:T(8,128)S(1)} async-done(((f32[64,32,256]{2,1,0:T(8,128)}), f32[64,32,256]{2,1,0:T(8,128)S(1)}, u32[]{:S(2)}, u32[]{:S(2)}) %all-to-all-start.2) | async-done | bytes 2097184 | tf_op jit(solution)/shard_map/all_to_all | solution.py:45
  521.5 12.5 %scatter_custom_fusion.1 = f32[2048,256]{1,0:T(8,128)S(1)} fusion(s32[2048]{0:T(1024)} %bitcast.62, f32[2048,256]{1,0:T(8,128)} %bitcast.51, f32[]{:T(128)} %constant.20.clone.1), kind=kCustom, calls=%fused_computation.30 | custom fusion | flops 524288 | bytes 2097664 | tf_op jit(solution)/shard_map/scatter-add | solution.py:172
  534.0 13.0 %scatter_custom_fusion.2 = f32[2048,256]{1,0:T(8,128)} fusion(s32[2048]{0:T(1024)S(1)} %bitcast.59, f32[2048,256]{1,0:T(8,128)S(1)} %scatter_custom_fusion.1, f32[]{:T(128)} %constant.20.clone.1), kind=kCustom, calls=%fused_computation.28 | custom fusion | flops 524288 | bytes 2097156 | tf_op jit(solution)/shard_map/scatter-add | solution.py:172
  546.9 13.3 %scatter_custom_fusion.3 = f32[2048,256]{1,0:T(8,128)} fusion(s32[2048]{0:T(1024)S(1)} %bitcast.56, f32[2048,256]{1,0:T(8,128)} %scatter_custom_fusion.2, f32[]{:T(128)} %constant.20.clone.1), kind=kCustom, calls=%fused_computation.26 | custom fusion | flops 524288 | bytes 2097664 | tf_op jit(solution)/shard_map/scatter-add | solution.py:172
  561.7 7.0 %all-to-all-start.3 = ((f32[64,1,256]{2,1,0:T(1,128)}), f32[64,1,256]{2,1,0:T(1,128)S(1)}, u32[]{:S(2)}, u32[]{:S(2)}) async-start(f32[64,1,256]{2,1,0:T(1,128)} %broadcast_in_dim.96), calls=%async_computation.3 | async-start | bytes 131072 | tf_op jit(solution)/shard_map/all_to_all | solution.py:45
  570.1 8.6 %all-to-all-done.3 = f32[64,1,256]{2,1,0:T(1,128)S(1)} async-done(((f32[64,1,256]{2,1,0:T(1,128)}), f32[64,1,256]{2,1,0:T(1,128)S(1)}, u32[]{:S(2)}, u32[]{:S(2)}) %all-to-all-start.3) | async-done | bytes 65568 | tf_op jit(solution)/shard_map/all_to_all | solution.py:45
  580.1 7.5 %all-reduce = (f32[]{:T(128)}, f32[]{:T(128)}) all-reduce(f32[]{:T(128)} %get-tuple-element.5, f32[]{:T(128)} %get-tuple-element.4), channel_id=1, replica_groups=mesh['leaf_0'=8,'leaf_1'=4,'leaf_2'=2,'hand'=4] {'hand'}, use_global_device_ids=true, to_apply=%region_12.14 | all-reduce | flops 2 | bytes 16 | tf_op jit(solution)/shard_map/psum | solution.py:179
  (75 shorter events, 15.4 us)
Async XLA Ops:
  7.2 55.3 %copy-start.15 = (s32[96,8]{0,1:T(8,128)S(1)}, s32[96,8]{0,1:T(8,128)}, u32[]{:S(2)}) copy-start(s32[96,8]{0,1:T(8,128)} %param.24) | copy-start | bytes 9220
  7.2 55.4 %copy-start.19 = (s32[96]{0:T(128)S(1)}, s32[96]{0:T(128)}, u32[]{:S(2)}) copy-start(s32[96]{0:T(128)} %param.22) | copy-start | bytes 1156
  7.2 56.0 %copy-start.14 = (s32[96,5]{0,1:T(8,128)S(1)}, s32[96,5]{0,1:T(8,128)}, u32[]{:S(2)}) copy-start(s32[96,5]{0,1:T(8,128)} %param.20) | copy-start | bytes 5764
  7.2 57.3 %copy-start.7 = (s32[3,2048]{1,0:T(4,128)S(1)}, s32[3,2048]{1,0:T(4,128)}, u32[]{:S(2)}) copy-start(s32[3,2048]{1,0:T(4,128)} %param.19) | copy-start | bytes 73732
  7.2 53.7 %all-gather.4.cloned.1.call-start = ((), (), s32[]{:S(2)}) async-start(), calls=%async_computation.4 | async-start | bytes 2359296 | tf_op jit(solution)/shard_map/all_gather | solution.py:21
  19.9 65.3 %all-gather.6.cloned.1.call-start = ((), (), s32[]{:S(2)}) async-start(), calls=%async_computation.5 | async-start | bytes 6291456 | tf_op jit(solution)/shard_map/all_gather | solution.py:21
  61.7 2.3 copy-start.8
  62.5 1.5 copy-start.10
  64.5 23.3 %copy-start.3 = (s32[1,2048]{1,0:T(1,128)}, s32[1,2048]{1,0:T(1,128)S(1)}, u32[]{:S(2)}) copy-start(s32[1,2048]{1,0:T(1,128)S(1)} %get-tuple-element.15) | copy-start | bytes 24580
  87.9 1.8 copy-start.16
  144.9 7.4 %copy-start.5 = (s32[96,8,8]{0,2,1:T(8,128)S(1)}, s32[96,8,8]{0,2,1:T(8,128)}, u32[]{:S(2)}) copy-start(s32[96,8,8]{0,2,1:T(8,128)} %param.26) | copy-start | bytes 73732
  144.9 7.5 %copy-start.4 = (s32[96,8,8]{0,2,1:T(8,128)S(1)}, s32[96,8,8]{0,2,1:T(8,128)}, u32[]{:S(2)}) copy-start(s32[96,8,8]{0,2,1:T(8,128)} %param.25) | copy-start | bytes 73732
  144.9 7.6 %copy-start.6 = (s32[96,1024]{1,0:T(8,128)S(1)}, s32[96,1024]{1,0:T(8,128)}, u32[]{:S(2)}) copy-start(s32[96,1024]{1,0:T(8,128)} %param.21) | copy-start | bytes 1179652
  144.9 7.6 %copy-start.18 = (s32[96]{0:T(128)S(1)}, s32[96]{0:T(128)}, u32[]{:S(2)}) copy-start(s32[96]{0:T(128)} %param.23) | copy-start | bytes 1156
  144.9 7.7 %copy-start.9 = (s32[256]{0:T(256)S(1)}, s32[256]{0:T(256)}, u32[]{:S(2)}) copy-start(s32[256]{0:T(256)} %copy-done.8) | copy-start | bytes 3076
  144.9 7.7 %copy-start.11 = (s32[256]{0:T(256)S(1)}, s32[256]{0:T(256)}, u32[]{:S(2)}) copy-start(s32[256]{0:T(256)} %copy-done.10) | copy-start | bytes 3076
  144.9 7.7 %copy-start.12 = (s32[1024]{0:T(1024)S(1)}, s32[1024]{0:T(1024)}, u32[]{:S(2)}) copy-start(s32[1024]{0:T(1024)} %constant.77.clone) | copy-start | bytes 12292
  144.9 7.7 %copy-start.13 = (s32[1024]{0:T(1024)S(1)}, s32[1024]{0:T(1024)}, u32[]{:S(2)}) copy-start(s32[1024]{0:T(1024)} %constant.78.clone) | copy-start | bytes 12292
  144.9 190.7 %all-to-all-start = ((bf16[96,64,1024]{0,1,2:T(8,128)(2,1)}), bf16[96,64,1024]{0,1,2:T(8,128)(2,1)}, u32[]{:S(2)}, u32[]{:S(2)}) async-start(bf16[96,64,1024]{0,1,2:T(8,128)(2,1)} %bitcast.47), calls=%async_computation | async-start | bytes 33554432 | tf_op jit(solution)/shard_map/all_to_all | solution.py:108
  360.6 8.5 %copy-start = (bf16[96,64,1024]{2,1,0:T(8,128)(2,1)S(1)}, bf16[96,64,1024]{2,1,0:T(8,128)(2,1)}, u32[]{:S(2)}) copy-start(bf16[96,64,1024]{2,1,0:T(8,128)(2,1)} %copy.49) | copy-start | bytes 37748740
  360.6 8.5 %copy-start.2 = (f32[96,256]{1,0:T(8,128)S(1)}, f32[96,256]{1,0:T(8,128)}, u32[]{:S(2)}) copy-start(f32[96,256]{1,0:T(8,128)} %get-tuple-element.18) | copy-start | bytes 294916
  463.4 56.7 %all-to-all-start.2 = ((f32[64,32,256]{2,1,0:T(8,128)}), f32[64,32,256]{2,1,0:T(8,128)S(1)}, u32[]{:S(2)}, u32[]{:S(2)}) async-start(f32[64,32,256]{2,1,0:T(8,128)} %broadcast_in_dim.59), calls=%async_computation.2 | async-start | bytes 4194304 | tf_op jit(solution)/shard_map/all_to_all | solution.py:45
  520.1 1.4 copy-start.1
  534.0 44.9 %copy-start.17 = (f32[256]{0:T(256)S(1)}, f32[256]{0:T(256)}, u32[]{:S(2)}) copy-start(f32[256]{0:T(256)} %param.17) | copy-start | bytes 3076
  561.7 17.0 %all-to-all-start.3 = ((f32[64,1,256]{2,1,0:T(1,128)}), f32[64,1,256]{2,1,0:T(1,128)S(1)}, u32[]{:S(2)}, u32[]{:S(2)}) async-start(f32[64,1,256]{2,1,0:T(1,128)} %broadcast_in_dim.96), calls=%async_computation.3 | async-start | bytes 131072 | tf_op jit(solution)/shard_map/all_to_all | solution.py:45
Sparse Core Ops, SparseCore 0:
  20.1 40.8 all-gather.3
  62.7 22.4 all-gather.5
